TPU v7x, 8 devices: a whole 2x2x1 slice. The times are simulated.
8 devices in a mesh: dp: 1 (over z), tp: 2 (over y), sp: 4 (over x, core).
Axes of the slice: x: 2, y: 2, z: 1, core: 2. Of those that a mesh axis runs over, the one named last changes fastest.
Arguments:
- hidden: bfloat16 [16, 1024], P('dp')
- k_cache: bfloat16 [16, 16384, 16, 64], P('dp', 'sp', 'tp')
- v_cache: bfloat16 [16, 16384, 16, 64], P('dp', 'sp', 'tp')
- lengths: int32 [16], P('dp')
- rel_table: bfloat16 [16384, 16, 64], P('sp', 'tp')
- u_bias: bfloat16 [16, 64], P('tp')
- w_bias: bfloat16 [16, 64], P('tp')
- g_attn: bfloat16 [1024], replicated
- w_query: bfloat16 [1024, 16, 64], P(None, 'tp')
- w_key: bfloat16 [1024, 16, 64], P(None, 'tp')
- w_value: bfloat16 [1024, 16, 64], P(None, 'tp')
- w_out: bfloat16 [16, 64, 1024], P('tp')
- g_mlp: bfloat16 [1024], replicated
- w_up: bfloat16 [1024, 4096], P(None, 'tp')
- w_down: bfloat16 [4096, 1024], P('tp')
Outputs:
- output: bfloat16 [16, 1024], P('dp')
All inputs are finite; a program needn't handle non-finite values.
Results may differ from a plain program's by a relative error of at most 0.0166655.
Values sent between devices are 32-bit elements.
A program may use at most 1 GiB of HBM per device.

v0:
```python
import functools

import jax
import jax.numpy as jnp
from jax import lax
from jax.experimental import pallas as pl
from jax.experimental.pallas import tpu as pltpu
from jax.sharding import PartitionSpec as P

EPS = 1e-6
MASKED = -1e30
MESH = pl.DeviceIdType.MESH
F32 = jnp.float32
BF16 = jnp.bfloat16
NT = (((1,), (1,)), ((), ()))
NS = 10
LATE = 4


def rms(x, gain):
    mean_sq = jnp.mean(x * x, axis=-1, keepdims=True)
    return (x * lax.rsqrt(mean_sq + EPS) * gain).astype(BF16)


def kernel(caps, hid_hbm, k_hbm, v_hbm, len_hbm, r_hbm, u_hbm, w_hbm, ga_hbm, wq_hbm, wk_hbm, wv_hbm, wo_hbm, gm_hbm, wu_hbm, wd_hbm,
           out_ref, flag_ref,
           hid_ref, len_ref, u_ref, w_ref, ga_ref, gm_ref, ring, rel_own, rel_par, content, probs, p_extra, wo, wu, wd, qc_bd, k_new, v_new, rows_acc, part_e, part_l, asend_e, arecv_e, asend_l, arecv_l, dsend_e, drecv_e, dsend_l, drecv_l,
           ring_sem, wt_sem, r_sem, par_sem, cro_send, cro_recv, dia_send, dia_recv, part_send, part_recv, att_sem, ex_send, ex_recv, table, *far_refs):
    nb, nh, width = content.shape
    feat = k_hbm.shape[1]
    hd = feat // nh
    even, odd = caps
    stages = len(even) - 1
    group = nb // stages
    compact = even[-1] < nb
    rel_cro, rel_dia = far_refs[:stages], far_refs[stages:2 * stages]
    rel_send = far_refs[-1] if compact else rel_own
    sp = lax.axis_index("sp")
    tp = lax.axis_index("tp")
    chip = sp // 2
    core = lax.rem(sp, 2)
    partner = chip * 2 + (1 - core)
    cross = (1 - chip) * 2 + core
    diag = (1 - chip) * 2 + (1 - core)

    def by_core(c, a, b):
        return a + (b - a) * c

    def size(g, c):
        return by_core(c, even[g + 1] - even[g], odd[g + 1] - odd[g])

    def begin(g, c):
        return by_core(c, even[g], odd[g])

    barrier = pltpu.get_barrier_semaphore()
    for peer in (partner, cross, diag):
        pl.semaphore_signal(barrier, inc=1, device_id={"sp": peer}, device_id_type=MESH)
    pl.semaphore_signal(barrier, inc=1, device_id={"tp": 1 - tp}, device_id_type=MESH)

    def load(src, dst, sem):
        return pltpu.make_async_copy(src, dst, sem)

    def k_load(b):
        return load(k_hbm.at[b], ring.at[lax.rem(b, NS)], ring_sem.at[lax.rem(b, NS)])

    def v_load(b):
        slot = lax.rem(b + nb, NS)
        return load(v_hbm.at[b], ring.at[slot], ring_sem.at[slot])

    small = [load(a, b, wt_sem.at[6 + i]) for i, (a, b) in enumerate(((hid_hbm, hid_ref), (ga_hbm, ga_ref), (len_hbm, len_ref), (u_hbm, u_ref), (w_hbm, w_ref), (gm_hbm, gm_ref)))]
    for copy in small:
        copy.start()
    wdt = wq_hbm.shape[1]
    stage = ring.at[NS - 2]
    step = 1024
    r_copies = [load(r_hbm.at[:, pl.ds(c, step)], ring.at[NS - 1, :, pl.ds(c, step)], r_sem.at[c // step]) for c in range(0, width, step)]
    wq_copy = load(wq_hbm, stage.at[:, pl.ds(0, wdt)], wt_sem.at[0])
    wk_copy = load(wk_hbm, stage.at[:, pl.ds(wdt, wdt)], wt_sem.at[1])
    wv_copy = load(wv_hbm, stage.at[:, pl.ds(2 * wdt, wdt)], wt_sem.at[2])
    wo_copy = load(wo_hbm, wo, wt_sem.at[3])
    wu_copy = load(wu_hbm, wu, wt_sem.at[4])
    wd_copy = load(wd_hbm, wd, wt_sem.at[5])
    wq_copy.start()
    for copy in r_copies:
        copy.start()
    wk_copy.start()
    wv_copy.start()
    for b in range(NS - 2):
        k_load(b).start()

    for copy in small:
        copy.wait()
    fits = jnp.int32(1)
    if compact:
        for level, cap in enumerate(caps):
            rank = jnp.int32(0)
            for b in range(nb):
                table[level, b] = rank
                rank = rank + (len_ref[b] >= (2 + level) * width).astype(jnp.int32)
                if (b + 1) % group == 0:
                    fits = jnp.where(rank <= cap[(b + 1) // group], fits, 0)
        reach = [len_ref[b] >= (2 + core) * width for b in range(nb)]
        ranks = [table[core, b] for b in range(nb)]
        chosen = {}
        for g in range(stages):
            for c in range(even[g + 1] - even[g]):
                want = begin(g, core) + c
                chosen[g, c] = functools.reduce(jnp.add, [jnp.where(reach[b] & (ranks[b] == want), b, 0) for b in range(nb)])

    flag_ref[0] = fits
    hidden = hid_ref[...].astype(F32)
    normed = rms(hidden, ga_ref[...][None].astype(F32))

    head_of_row = lax.broadcasted_iota(jnp.int32, (nh, feat), 0)
    head_of_col = lax.broadcasted_iota(jnp.int32, (nh, feat), 1) // hd
    diag_mask = head_of_row == head_of_col
    spread_row = lax.broadcasted_iota(jnp.int32, (hd, feat), 0)
    spread_col = lax.rem(lax.broadcasted_iota(jnp.int32, (hd, feat), 1), hd)
    spread = (spread_row == spread_col).astype(BF16)
    u_wide = jnp.dot(u_ref[...], spread, preferred_element_type=F32)
    w_wide = jnp.dot(w_ref[...], spread, preferred_element_type=F32)

    wq_copy.wait()
    query = lax.dot_general(normed, stage[:, pl.ds(0, wdt)], NT, preferred_element_type=F32).astype(BF16).astype(F32)
    zero_rows = jnp.zeros((nh, feat), F32)
    pos_rows = []
    for b in range(nb):
        row = query[b:b + 1, :]
        qc = jnp.where(diag_mask, row + u_wide, 0.0)
        qc_bd[b] = jnp.concatenate([qc, zero_rows], axis=0).astype(BF16)
        pos_rows.append(jnp.where(diag_mask, row + w_wide, 0.0))
    q_pos = jnp.concatenate(pos_rows, axis=0).astype(BF16)

    for c in range(width // step):
        cols = pl.ds(c * step, step)
        r_copies[c].wait()
        prod = jnp.dot(q_pos, ring[NS - 1, :, cols], preferred_element_type=F32)
        rel_own[:, :, cols] = prod.reshape(nb, nh, step)
    pl.semaphore_wait(barrier, 4)

    par_copy = pltpu.make_async_remote_copy(src_ref=rel_own, dst_ref=rel_par, send_sem=par_sem.at[0], recv_sem=par_sem.at[1],
                                            device_id={"sp": partner}, device_id_type=MESH)

    def cross_copy(g, c):
        i = even[g] + c
        return pltpu.make_async_remote_copy(src_ref=rel_send.at[i], dst_ref=rel_cro[g].at[c], send_sem=cro_send.at[i], recv_sem=cro_recv.at[i],
                                            device_id={"sp": cross}, device_id_type=MESH)

    def forward_copy(g, c):
        i = even[g] + c
        return pltpu.make_async_remote_copy(src_ref=rel_cro[g].at[c], dst_ref=rel_dia[g].at[c], send_sem=dia_send.at[i], recv_sem=dia_recv.at[i],
                                            device_id={"sp": partner}, device_id_type=MESH)

    for g in range(stages):
        for c in range(even[g + 1] - even[g]):
            if compact:
                rel_send[even[g] + c] = rel_own[chosen[g, c]]

            @pl.when(c < size(g, core))
            def _():
                cross_copy(g, c).start()
        if g == 0:
            par_copy.start()

    wk_copy.wait()
    k_new[...] = lax.dot_general(normed, stage[:, pl.ds(wdt, wdt)], NT, preferred_element_type=F32).astype(BF16).astype(F32)
    wv_copy.wait()
    v_new[...] = lax.dot_general(normed, stage[:, pl.ds(2 * wdt, wdt)], NT, preferred_element_type=F32).astype(BF16).astype(F32)
    for b in range(NS - 2, NS):
        k_load(b).start()

    def arrive(g, c):
        @pl.when((c >= 0) & (c < size(g, core)))
        def _():
            cross_copy(g, c).wait()
            forward_copy(g, c).start()

    @pl.loop(0, nb)
    def _(b):
        @pl.when(b == nb - 3)
        def _():
            for c in range(rel_cro[0].shape[0]):
                arrive(0, c)

        k_load(b).wait()
        content[b] = jnp.dot(qc_bd[b], ring[lax.rem(b, NS)], preferred_element_type=F32)[:nh]

        @pl.when(b < nb - NS)
        def _():
            k_load(b + NS).start()

        @pl.when(b >= nb - NS)
        def _():
            v_load(b + NS - nb).start()

    wo_copy.start()
    par_copy.wait()

    lane = lax.broadcasted_iota(jnp.int32, (nh, width), 1)
    back = 127 - lax.broadcasted_iota(jnp.int32, (nh, 128), 1)
    stat_lane = lax.broadcasted_iota(jnp.int32, (nh, 128), 1)
    stat_row = lax.broadcasted_iota(jnp.int32, (nh, 128), 0)

    def pick(rows, g, b, level):
        if not compact:
            return rows[g][b - g * group]
        unit = table[level, b]
        x = rows[0][jnp.minimum(unit, rows[0].shape[0] - 1)]
        for h in range(1, g + 1):
            local = unit - begin(h, level)
            x = jnp.where(local >= 0, rows[h][jnp.clip(local, 0, rows[h].shape[0] - 1)], x)
        return x

    def score(g, b, slot):
        length = len_ref[b]
        high = length // width
        low = length - high * width
        first = high - sp
        upper = lane <= low
        far = pick(rel_cro, g, b, core)
        farther = pick(rel_dia, g, b, 1 - core)
        comb = jnp.zeros((nh, width), F32)
        for block, rows in ((sp, rel_own[b]), (partner, rel_par[b]), (cross, far), (diag, farther)):
            want = jnp.where(upper, first, first - 1) == block
            comb = jnp.where(want, rows, comb)
        pieces = [jnp.take_along_axis(comb[:, 128 * c:128 * c + 128], back, axis=1) for c in range(width // 128)]
        relative = pltpu.roll(jnp.concatenate(pieces[::-1], axis=1), lax.rem(low + 1, width), axis=1)
        here = length - sp * width
        valid = lane <= here
        is_new = lane == here
        q_rows = qc_bd[b][:nh].astype(F32)
        s_new = jnp.sum(q_rows * k_new[pl.ds(b, 1), :], axis=1, keepdims=True)
        scores = jnp.where(is_new, s_new, content[b]) + relative
        scores = jnp.where(valid, scores * (hd ** -0.5), MASKED)
        top = jnp.max(scores, axis=1, keepdims=True)
        weights = jnp.where(valid, jnp.exp(scores - top), 0.0)
        total = jnp.sum(weights, axis=1, keepdims=True)
        p_new = jnp.sum(jnp.where(is_new, weights, 0.0), axis=1, keepdims=True).astype(BF16).astype(F32)
        probs[slot] = jnp.where(is_new, 0.0, weights).astype(BF16)
        p_extra[slot] = jnp.broadcast_to(p_new, (nh, 128))
        stats = jnp.where(stat_lane == stat_row, top, jnp.where(stat_lane == stat_row + nh, total, 0.0))
        rows_acc[b, :, pl.ds(feat, 128)] = jnp.sum(stats, axis=0, keepdims=True)

    def mix(b, slot):
        mixed = lax.dot_general(probs[slot], ring[lax.rem(b + nb, NS)], NT, preferred_element_type=F32)
        mixed = mixed + p_extra[slot][:, :1] * v_new[pl.ds(b, 1), :]
        rows_acc[b, :, pl.ds(0, feat)] = jnp.sum(jnp.where(diag_mask, mixed, 0.0), axis=0, keepdims=True)

    def settle(g):
        for c in range(rel_cro[g].shape[0]):
            @pl.when(c < size(g, core))
            def _():
                forward_copy(g, c).wait_send()

            @pl.when(c < size(g, 1 - core))
            def _():
                forward_copy(g, c).wait_recv()

    settle(0)
    score(0, 0, 0)

    lane_heads = [lax.broadcasted_iota(jnp.int32, (8, 128), 1) // hd + c * (128 // hd) for c in range(feat // 128)]

    def peers(part, k):
        return [pltpu.make_async_remote_copy(src_ref=part.at[0], dst_ref=part.at[j], send_sem=part_send.at[k, j], recv_sem=part_recv.at[k, j],
                                             device_id={"sp": peer}, device_id_type=MESH) for j, peer in ((1, partner), (2, cross), (3, diag))]

    def share(part, k, base):
        for b in range(part.shape[1]):
            part[0, b:b + 1, :] = rows_acc[base + b]
        for copy in peers(part, k):
            copy.start()

    def exchange(send, recv, k):
        return pltpu.make_async_remote_copy(src_ref=send, dst_ref=recv, send_sem=att_sem.at[k, 0], recv_sem=att_sem.at[k, 1],
                                            device_id={"tp": 1 - tp}, device_id_type=MESH)

    def merge(part, k):
        for copy in peers(part, k):
            copy.wait()
        blocks = []
        for s in range(4):
            j = lax.rem(chip + s // 2, 2) * 2 + lax.rem(core + s % 2, 2)
            blocks.append(part[j])
        tops = [x[:, feat:] for x in blocks]
        top_all = functools.reduce(jnp.maximum, tops)
        scale = [jnp.exp(t - top_all) for t in tops]
        total = sum(s * pltpu.roll(t, 128 - nh, axis=1) for s, t in zip(scale, tops))
        context = jnp.zeros((part.shape[1], feat), F32)
        for s, x in zip(scale, blocks):
            factor = s / total
            wide = jnp.concatenate([sum(jnp.where(lane_heads[c][:1] == h, factor[:, h:h + 1], 0.0) for h in range(c * (128 // hd), (c + 1) * (128 // hd))) for c in range(feat // 128)], axis=1)
            context = context + wide * x[:, :feat]
        return jnp.dot(context.astype(BF16), wo[...], preferred_element_type=F32)

    def finish_early():
        wo_copy.wait()
        asend_e[...] = merge(part_e, 0)
        exchange(asend_e, arecv_e, 0).start()

    for g in range(stages):
        late = rel_cro[g + 1].shape[0] if g + 1 < stages else 0
        first_step = max(g * group - 1, 0)
        last_step = g * group + group - 2
        if g > 0:
            settle(g)
        for c in range(late - (last_step - first_step + 1)):
            arrive(g + 1, c)

        @pl.loop(first_step, last_step + 1)
        def _(i):
            if late:
                arrive(g + 1, i - last_step + late - 1)

            if g == stages - 1:
                @pl.when(i == nb - LATE)
                def _():
                    share(part_e, 0, 0)

            v_load(i).wait()
            mix(i, lax.rem(i, 2))
            score(g, i + 1, lax.rem(i + 1, 2))

            @pl.when(i < nb - NS)
            def _():
                v_load(i + NS).start()

    wu_copy.start()
    wd_copy.start()
    v_load(nb - 1).wait()
    mix(nb - 1, (nb - 1) % 2)

    def down_copies(send, recv, k):
        return [pltpu.make_async_remote_copy(src_ref=send.at[c], dst_ref=recv.at[c], send_sem=ex_send.at[k, c], recv_sem=ex_recv.at[k, c],
                                             device_id={"tp": 1 - tp}, device_id_type=MESH) for c in range(send.shape[0])]

    def mlp(rows, attn, send, recv, k):
        middle = (rows + attn).astype(BF16).astype(F32)
        normed_mlp = rms(middle, gm_ref[...][None].astype(F32))
        up = jnp.dot(normed_mlp, wu[...], preferred_element_type=F32)
        act = jax.nn.gelu(up, approximate=True).astype(BF16)
        cols = send.shape[2]
        for c, copy in enumerate(down_copies(send, recv, k)):
            send[c] = jnp.dot(act, wd[:, c * cols:(c + 1) * cols], preferred_element_type=F32)
            copy.start()
        return middle

    def finish(middle, send, recv, k):
        done = []
        cols = send.shape[2]
        for c, copy in enumerate(down_copies(send, recv, k)):
            copy.wait()
            done.append(middle[:, c * cols:(c + 1) * cols] + (send[c] + recv[c]))
        return jnp.concatenate(done, axis=1)

    cut = nb - LATE
    share(part_l, 1, cut)
    finish_early()
    asend_l[...] = merge(part_l, 1)
    exchange(asend_l, arecv_l, 1).start()
    exchange(asend_e, arecv_e, 0).wait()
    wu_copy.wait()
    wd_copy.wait()
    middle_e = mlp(hidden[:cut], asend_e[...] + arecv_e[...], dsend_e, drecv_e, 0)
    exchange(asend_l, arecv_l, 1).wait()
    middle_l = mlp(hidden[cut:], asend_l[...] + arecv_l[...], dsend_l, drecv_l, 1)
    first = finish(middle_e, dsend_e, drecv_e, 0)
    last = finish(middle_l, dsend_l, drecv_l, 1)
    out_ref[...] = jnp.concatenate([first, last], axis=0).astype(BF16)


def solution(mesh):
    spec_cache = P('dp', 'sp', 'tp', None)
    in_specs = (P('dp', None), spec_cache, spec_cache, P('dp'), P('sp', 'tp', None), P('tp', None), P('tp', None), P(None), P(None, 'tp', None), P(None, 'tp', None), P(None, 'tp', None), P('tp', None, None), P(None), P(None, 'tp'), P('tp', None))

    def layer_step(hidden, k_cache, v_cache, lengths, rel_table, u_bias, w_bias, g_attn, w_query, w_key, w_value, w_out, g_mlp, w_up, w_down):
        nb, width, nh, hd = k_cache.shape
        feat = nh * hd
        model = hidden.shape[1]
        k_t = k_cache.transpose(0, 2, 3, 1).reshape(nb, feat, width)
        v_t = v_cache.transpose(0, 2, 3, 1).reshape(nb, feat, width)
        r_t = rel_table.transpose(1, 2, 0).reshape(feat, width)
        proj = [w.transpose(1, 2, 0).reshape(feat, model) for w in (w_query, w_key, w_value)]
        vmem = pl.BlockSpec(memory_space=pltpu.VMEM)
        hbm = pl.BlockSpec(memory_space=pl.ANY)
        dma = pltpu.SemaphoreType.DMA
        full = 2 * ((0, nb),)
        tight = (0, 4, 7, 10, 13), (0, 3, 5, 7, 8)

        def call(caps, *operands):
            compact = caps != full
            rows = caps[0][-1]
            return pl.pallas_call(
                functools.partial(kernel, caps),
                out_shape=(jax.ShapeDtypeStruct((nb, model), BF16), jax.ShapeDtypeStruct((1,), jnp.int32)),
                in_specs=15 * [hbm],
                out_specs=(vmem, pl.BlockSpec(memory_space=pltpu.SMEM)),
                scratch_shapes=[
                    pltpu.VMEM(hidden.shape, BF16),
                    pltpu.SMEM(lengths.shape, jnp.int32),
                    pltpu.VMEM(u_bias.shape, BF16),
                    pltpu.VMEM(w_bias.shape, BF16),
                    pltpu.VMEM(g_attn.shape, BF16),
                    pltpu.VMEM(g_mlp.shape, BF16),
                    pltpu.VMEM((NS, feat, width), BF16),
                    pltpu.VMEM((nb, nh, width), F32),
                    pltpu.VMEM((nb, nh, width), F32),
                    pltpu.VMEM((nb, nh, width), F32),
                    pltpu.VMEM((2, nh, width), BF16),
                    pltpu.VMEM((2, nh, 128), F32),
                    pltpu.VMEM((feat, model), BF16),
                    pltpu.VMEM(w_up.shape, BF16),
                    pltpu.VMEM(w_down.shape, BF16),
                    pltpu.VMEM((nb, 16, feat), BF16),
                    pltpu.VMEM((nb, feat), F32),
                    pltpu.VMEM((nb, feat), F32),
                    pltpu.VMEM((nb, 1, feat + 128), F32),
                    pltpu.VMEM((4, nb - LATE, feat + 128), F32),
                    pltpu.VMEM((4, LATE, feat + 128), F32),
                    pltpu.VMEM((nb - LATE, model), F32),
                    pltpu.VMEM((nb - LATE, model), F32),
                    pltpu.VMEM((LATE, model), F32),
                    pltpu.VMEM((LATE, model), F32),
                    pltpu.VMEM((2, nb - LATE, model // 2), F32),
                    pltpu.VMEM((2, nb - LATE, model // 2), F32),
                    pltpu.VMEM((2, LATE, model // 2), F32),
                    pltpu.VMEM((2, LATE, model // 2), F32),
                    dma((NS,)), dma((12,)), dma((4,)), dma((2,)), dma((rows,)), dma((rows,)), dma((rows,)), dma((rows,)), dma((2, 4)), dma((2, 4)), dma((2, 2)), dma((2, 2)), dma((2, 2)),
                    pltpu.SMEM((2, nb), jnp.int32),
                ] + 2 * [pltpu.VMEM((b - a, nh, width), F32) for a, b in zip(caps[0], caps[0][1:])] + ([pltpu.VMEM((rows, nh, width), F32)] if compact else []),
                compiler_params=pltpu.CompilerParams(collective_id=int(compact), has_side_effects=True, vmem_limit_bytes=67043328),
            )(*operands)

        operands = (hidden, k_t, v_t, lengths, r_t, u_bias, w_bias, g_attn, *proj, w_out.reshape(feat, model), g_mlp, w_up, w_down)
        out, fits = call(tight, *operands)
        return lax.cond(fits[0] > 0, lambda *_: out, lambda *full_operands: call(full, *full_operands)[0], *operands)

    return jax.shard_map(layer_step, mesh=mesh, in_specs=in_specs, out_specs=P('dp', None), check_vma=False)
```

profile of v0, /device:TPU:0, one launch (start us, length us, event | category | flops | bytes accessed | tf_op | source)
XLA Modules:
  0.0 60.4 jit_solution(14409888307057385429)
XLA Ops:
  0.0 58.3 %shard_map.147 = (bf16[16,1024]{1,0:T(8,128)(2,1)}, s32[1]{0:T(128)}) custom-call(bf16[16,1024]{1,0:T(8,128)(2,1)} %hid_hbm.1, bf16[16,512,4096]{2,1,0:T(8,128)(2,1)} %bitcast.1.k_hbm, bf16[16,512,4096]{2,1,0:T(8,128)(2,1)} %bitcast.3.v_hbm, s32[16]{0:T(128)} %len_hbm.1, bf16[512,4096]{1,0:T(8,128)(2,1)} %bitcast.20, bf16[8,64]{1,0:T(8,128)(2,1)} %u_hbm.1, ...), custom_call_target="tpu_custom_call" | custom-call | tf_op jit(solution)/shard_map/pallas_call | solution.py:393
  58.9 0.2 conditional.1
  59.1 1.4 %copy.21 = bf16[16,1024]{1,0:T(8,128)(2,1)} copy(bf16[16,1024]{1,0:T(8,128)(2,1)} %get-tuple-element.59) | data formatting | bytes 65536
where the time goes:
time: 60.6 us; the launch traced here: 60.4 us
  Pallas kernels  58.3 us (96%)
  local copies, waits for them, and re-layouts  1.38 us (2%)
    pallas_call x1, Pallas kernels, call(): pl.pallas_call(functools.partial(kernel, caps), out_shape=(jax.ShapeDtype...  58.3 us
    unnamed x1, local copies, waits for them, and re-layouts  1.38 us

commit v1 on v0

--- a/solution.py
+++ b/solution.py
@@ -13,7 +13,7 @@
 F32 = jnp.float32
 BF16 = jnp.bfloat16
 NT = (((1,), (1,)), ((), ()))
-NS = 10
+NS = 8
 LATE = 4
 
 
@@ -67,7 +67,12 @@
         slot = lax.rem(b + nb, NS)
         return load(v_hbm.at[b], ring.at[slot], ring_sem.at[slot])
 
-    small = [load(a, b, wt_sem.at[6 + i]) for i, (a, b) in enumerate(((hid_hbm, hid_ref), (ga_hbm, ga_ref), (len_hbm, len_ref), (u_hbm, u_ref), (w_hbm, w_ref), (gm_hbm, gm_ref)))]
+    if compact:
+        pairs = (hid_hbm, hid_ref), (ga_hbm, ga_ref), (len_hbm, len_ref), (u_hbm, u_ref), (w_hbm, w_ref), (gm_hbm, gm_ref)
+        small = [load(a, b, wt_sem.at[6 + i]) for i, (a, b) in enumerate(pairs)]
+    else:
+        small = []
+        hid_ref, ga_ref, len_ref, u_ref, w_ref, gm_ref = hid_hbm, ga_hbm, len_hbm, u_hbm, w_hbm, gm_hbm
     for copy in small:
         copy.start()
     wdt = wq_hbm.shape[1]
@@ -321,9 +326,10 @@
             mix(i, lax.rem(i, 2))
             score(g, i + 1, lax.rem(i + 1, 2))
 
-            @pl.when(i < nb - NS)
-            def _():
-                v_load(i + NS).start()
+            if first_step < nb - NS:
+                @pl.when(i < nb - NS)
+                def _():
+                    v_load(i + NS).start()
 
     wu_copy.start()
     wd_copy.start()
@@ -383,6 +389,8 @@
         proj = [w.transpose(1, 2, 0).reshape(feat, model) for w in (w_query, w_key, w_value)]
         vmem = pl.BlockSpec(memory_space=pltpu.VMEM)
         hbm = pl.BlockSpec(memory_space=pl.ANY)
+        smem = pl.BlockSpec(memory_space=pltpu.SMEM)
+        large = 1, 2, 4, 8, 9, 10, 11, 13, 14
         dma = pltpu.SemaphoreType.DMA
         full = 2 * ((0, nb),)
         tight = (0, 4, 7, 10, 13), (0, 3, 5, 7, 8)
@@ -393,7 +401,7 @@
             return pl.pallas_call(
                 functools.partial(kernel, caps),
                 out_shape=(jax.ShapeDtypeStruct((nb, model), BF16), jax.ShapeDtypeStruct((1,), jnp.int32)),
-                in_specs=15 * [hbm],
+                in_specs=[hbm if compact or i in large else smem if i == 3 else vmem for i in range(15)],
                 out_specs=(vmem, pl.BlockSpec(memory_space=pltpu.SMEM)),
                 scratch_shapes=[
                     pltpu.VMEM(hidden.shape, BF16),
@@ -428,7 +436,7 @@
                     dma((NS,)), dma((12,)), dma((4,)), dma((2,)), dma((rows,)), dma((rows,)), dma((rows,)), dma((rows,)), dma((2, 4)), dma((2, 4)), dma((2, 2)), dma((2, 2)), dma((2, 2)),
                     pltpu.SMEM((2, nb), jnp.int32),
                 ] + 2 * [pltpu.VMEM((b - a, nh, width), F32) for a, b in zip(caps[0], caps[0][1:])] + ([pltpu.VMEM((rows, nh, width), F32)] if compact else []),
-                compiler_params=pltpu.CompilerParams(collective_id=int(compact), has_side_effects=True, vmem_limit_bytes=67043328),
+                compiler_params=pltpu.CompilerParams(collective_id=int(compact), has_side_effects=True, vmem_limit_bytes=(57 if compact else 63) * 2 ** 20),
             )(*operands)
 
         operands = (hidden, k_t, v_t, lengths, r_t, u_bias, w_bias, g_attn, *proj, w_out.reshape(feat, model), g_mlp, w_up, w_down)

time: 60.6 us -> 59.8 us (0.987)
  local copies, waits for them, and re-layouts: 1.38 us -> 0.64 us
    unnamed x1 -> x13, local copies, waits for them, and re-layouts: 1.38 us -> 0.64 us
where the time goes in v1:
time: 59.8 us; the launch traced here: 59.7 us
  Pallas kernels  58.2 us (97%)
  between operations  0.7 us (1%)
  local copies, waits for them, and re-layouts  0.64 us (1%)
    pallas_call x1, Pallas kernels, call(): pl.pallas_call(functools.partial(kernel, caps), out_shape=(jax.ShapeDtype...  58.2 us

profile of v1, /device:TPU:0, one launch (start us, length us, event | category | flops | bytes accessed | tf_op | source)
XLA Modules:
  0.0 59.7 jit_solution(17492393297444910078)
XLA Ops:
  0.0 0.0 copy-start
  0.0 0.0 copy-start.1
  0.0 0.0 copy-start.2
  0.0 0.0 copy-start.3
  0.0 0.0 copy-start.4
  0.0 0.0 copy-start.5
  0.0 58.2 %shard_map.147 = (bf16[16,1024]{1,0:T(8,128)(2,1)S(1)}, s32[1]{0:T(128)}) custom-call(bf16[16,1024]{1,0:T(8,128)(2,1)} %hid_hbm.1, bf16[16,512,4096]{2,1,0:T(8,128)(2,1)} %bitcast.1.k_hbm, bf16[16,512,4096]{2,1,0:T(8,128)(2,1)} %bitcast.3.v_hbm, s32[16]{0:T(128)} %len_hbm.1, bf16[512,4096]{1,0:T(8,128)(2,1)} %bitcast.20, bf16[8,64]{1,0:T(8,128)(2,1)} %u_hbm.1, ...), custom_call_target="tpu_custom_call" | custom-call | tf_op jit(solution)/shard_map/pallas_call | solution.py:401
  58.8 0.0 copy-done
  58.9 0.0 copy-done.1
  58.9 0.0 copy-done.2
  58.9 0.0 copy-done.3
  58.9 0.0 copy-done.4
  58.9 0.0 copy-done.5
  58.9 0.2 conditional.1
  59.1 0.6 %copy.21 = bf16[16,1024]{1,0:T(8,128)(2,1)} copy(bf16[16,1024]{1,0:T(8,128)(2,1)S(1)} %get-tuple-element.59) | data formatting | bytes 65536
Async XLA Ops:
  0.0 58.8 %copy-start = (bf16[16,1024]{1,0:T(8,128)(2,1)S(1)}, bf16[16,1024]{1,0:T(8,128)(2,1)}, u32[]{:S(2)}) copy-start(bf16[16,1024]{1,0:T(8,128)(2,1)} %hid_hbm.1) | copy-start | bytes 98308
  0.0 58.9 %copy-start.1 = (bf16[8,64]{1,0:T(8,128)(2,1)S(1)}, bf16[8,64]{1,0:T(8,128)(2,1)}, u32[]{:S(2)}) copy-start(bf16[8,64]{1,0:T(8,128)(2,1)} %u_hbm.1) | copy-start | bytes 3076
  0.0 58.9 %copy-start.2 = (bf16[8,64]{1,0:T(8,128)(2,1)S(1)}, bf16[8,64]{1,0:T(8,128)(2,1)}, u32[]{:S(2)}) copy-start(bf16[8,64]{1,0:T(8,128)(2,1)} %w_hbm.1) | copy-start | bytes 3076
  0.0 58.9 %copy-start.3 = (bf16[1024]{0:T(1024)(128)(2,1)S(1)}, bf16[1024]{0:T(1024)(128)(2,1)}, u32[]{:S(2)}) copy-start(bf16[1024]{0:T(1024)(128)(2,1)} %ga_hbm.1) | copy-start | bytes 6148
  0.0 58.9 %copy-start.4 = (bf16[1024]{0:T(1024)(128)(2,1)S(1)}, bf16[1024]{0:T(1024)(128)(2,1)}, u32[]{:S(2)}) copy-start(bf16[1024]{0:T(1024)(128)(2,1)} %gm_hbm.1) | copy-start | bytes 6148
  0.0 58.9 %copy-start.5 = (s32[16]{0:T(128)S(1)}, s32[16]{0:T(128)}, u32[]{:S(2)}) copy-start(s32[16]{0:T(128)} %len_hbm.1) | copy-start | bytes 196
